TPU v7x, 32 devices: a whole 2x2x4 slice. The times are simulated.
32 devices in a mesh: groups: 2 (over x), freq: 8 (over z, y), gvec: 2 (over core).
Axes of the slice: x: 2, y: 2, z: 4, core: 2. Of those that a mesh axis runs over, the one named last changes fastest.
Arguments:
- screened: bfloat16 [16, 3072, 3072], P(('groups', 'freq'), 'gvec'), parts along dimension 0, may hold values from -0.109375 to 0.109375
- densities: bfloat16 [6144, 512], P(('groups', 'gvec'), 'freq'), parts along dimension 0, may hold values from -0.8046875 to 0.8046875
- pair_order: int32 [512], replicated, may hold values from 0 to 511, each once
- quad_index: int32 [4, 8], replicated, may hold values from 0 to 63
- quad_table: float32 [64], replicated, may hold values from 0.05 to 0.5
Outputs:
- kernel_out: float32 [8, 512, 512], P('groups', 'freq', 'gvec'), parts along dimension 0
There are 2 independent parts, one for each index of `groups`. A program takes and returns all parts, laid end to end along the dimension named above; an argument that names none is the same for every part. Nothing has to cross between parts.
All inputs are finite; a program needn't handle non-finite values.
Results may differ from a plain program's by a relative error of at most 0.0029.
Values may be sent and summed in bfloat16 or wider, within the bound.
A program may use at most 64 MiB of HBM per device.

v0:
```python
import jax
import jax.numpy as jnp
from jax import lax
from jax.sharding import PartitionSpec as P


def body(screened, densities, pair_order, quad_index, quad_table):
    screen = screened[0]
    own_rows = lax.all_gather(densities, "freq", axis=1, tiled=True)
    own_rows = jnp.take(own_rows, pair_order, axis=1)
    product = jnp.dot(
        screen,
        lax.all_gather(own_rows, "gvec", axis=0, tiled=True),
        preferred_element_type=jnp.float32,
    )
    product = product.astype(jnp.bfloat16)
    kernel = lax.dot_general(
        own_rows, product, (((0,), (0,)), ((), ())), preferred_element_type=jnp.float32
    )
    table_size = quad_table.shape[0]
    onehot = (
        quad_index[:, :, None] == jnp.arange(table_size, dtype=jnp.int32)[None, None, :]
    ).astype(jnp.float32)
    weights = jnp.sum(onehot * quad_table[None, None, :], axis=2)
    halves = lax.psum_scatter(kernel, "gvec", scatter_dimension=1, tiled=True)
    return jnp.einsum(
        "of,fij->oij",
        weights,
        lax.all_to_all(halves[None], "freq", split_axis=1, concat_axis=0, tiled=True),
        precision=lax.Precision.HIGHEST,
    )


def solution(mesh):
    placed = (P(("groups", "freq"), "gvec", None), P(("groups", "gvec"), "freq"), P(), P(), P())
    return jax.shard_map(
        body, mesh=mesh, in_specs=placed, out_specs=P("groups", "freq", "gvec"), check_vma=False
    )
```

profile of v0, /device:TPU:0, one launch (start us, length us, event | category | flops | bytes accessed | tf_op | source)
XLA Modules:
  0.0 126.2 jit_solution(10194464482765181643)
XLA Ops:
  6.5 0.0 all-gather.3.cloned.1.call-start
  6.5 0.7 all-gather.3.cloned.1.call-update
  7.3 0.0 all-gather.5.cloned.1.call-start
  7.3 0.7 compare_select_fusion
  8.0 0.7 compare_and_fusion
  8.7 47.8 %all-gather.3.cloned.1.call-done = bf16[1536,512]{0,1:T(8,128)(2,1)} async-done(((bf16[1536,64]{0,1:T(8,128)(2,1)}), bf16[1536,512]{0,1:T(8,128)(2,1)}) %all-gather.3.cloned.1.call-update) | async-done | bytes 1572880 | tf_op jit(solution)/shard_map/all_gather | solution.py:9
  56.5 5.2 %gather_fusion = bf16[512,1536]{1,0:T(8,128)(2,1)S(1)} fusion(bf16[1536,512]{0,1:T(8,128)(2,1)} %all-gather.3.cloned.1.call-done, s32[1024]{0:T(1024)S(1)} %pad_clamp_fusion), kind=kCustom, calls=%fused_computation | custom fusion | bytes 3147776 | tf_op jit(solution)/shard_map/jit(_take)/gather | solution.py:10
  61.7 1.4 %fusion.6 = bf16[1536,512]{0,1:T(8,128)(2,1)} fusion(bf16[512,1536]{1,0:T(8,128)(2,1)S(1)} %gather_fusion, pred[512]{0:T(512)(128)(4,1)S(1)} %compare_and_fusion), kind=kLoop, calls=%fused_computation.6 | loop fusion | flops 786432 | bytes 3146240 | tf_op jit(solution)/shard_map/jit(_take)/select_n | solution.py:10
  63.0 0.0 all-gather.5.cloned.1.call-update
  63.1 0.0 reduce-scatter.2.cloned.1.call-start
  63.1 10.6 %all-gather.5.cloned.1.call-done = bf16[3072,512]{0,1:T(8,128)(2,1)} async-done(((bf16[1536,512]{0,1:T(8,128)(2,1)}), bf16[3072,512]{0,1:T(8,128)(2,1)}) %all-gather.5.cloned.1.call-update) | async-done | bytes 3145744 | tf_op jit(solution)/shard_map/all_gather | solution.py:13
  73.7 11.5 %fusion.5 = f32[512,512]{1,0:T(8,128)} fusion(bf16[512,1536]{1,0:T(8,128)(2,1)S(1)} %gather_fusion, pred[512]{0:T(512)(128)(4,1)S(1)} %compare_and_fusion, bf16[3072,512]{0,1:T(8,128)(2,1)} %all-gather.5.cloned.1.call-done, bf16[1,1536,3072]{2,1,0:T(8,128)(2,1)} %param.5), kind=kOutput, calls=%fused_computation.5 | convolution fusion | flops 5638717440 | bytes 15204864 | tf_op jit(solution)/shard_map/dot_general | solution.py:17
  85.2 0.0 copy-start
  85.2 0.0 copy-start.1
  85.2 0.0 reduce-scatter.2.cloned.1.call-update
  85.2 9.7 %reduce-scatter.2.cloned.1.call-done = f32[512,256]{1,0:T(8,128)} async-done(((f32[512,512]{1,0:T(8,128)}), f32[512,256]{1,0:T(8,128)}) %reduce-scatter.2.cloned.1.call-update) | async-done | bytes 524304 | tf_op jit(solution)/shard_map/reduce_scatter | solution.py:25
  95.0 2.4 %copy.13 = f32[1,512,256]{2,0,1:T(1,128)} copy(f32[1,512,256]{2,1,0:T(8,128)} %bitcast.16) | data formatting | bytes 1048576 | tf_op jit(solution)/shard_map/broadcast_in_dim | solution.py:29
  97.3 5.8 %all-to-all-start = ((f32[1,512,256]{2,0,1:T(1,128)}), f32[1,512,256]{2,0,1:T(1,128)S(1)}, u32[]{:S(2)}, u32[]{:S(2)}) async-start(f32[1,512,256]{2,0,1:T(1,128)} %copy.13), calls=%async_computation.1 | async-start | bytes 1048576 | tf_op jit(solution)/shard_map/all_to_all | solution.py:29
  103.1 0.0 copy-done
  103.1 0.0 copy-done.1
  103.1 0.2 select_reduce_fusion
  103.3 14.8 %all-to-all-done = f32[1,512,256]{2,0,1:T(1,128)S(1)} async-done(((f32[1,512,256]{2,0,1:T(1,128)}), f32[1,512,256]{2,0,1:T(1,128)S(1)}, u32[]{:S(2)}, u32[]{:S(2)}) %all-to-all-start) | async-done | bytes 524320 | tf_op jit(solution)/shard_map/all_to_all | solution.py:29
  118.1 0.8 fusion.9
  118.9 0.8 copy.15
  (2 shorter events, 0.0 us)
Async XLA Ops:
  6.5 49.9 %all-gather.3.cloned.1.call-start = ((), (), s32[]{:S(2)}) async-start(), calls=%async_computation.2 | async-start | bytes 1769472 | tf_op jit(solution)/shard_map/all_gather | solution.py:9
  7.3 66.4 %all-gather.5.cloned.1.call-start = ((), (), s32[]{:S(2)}) async-start(), calls=%async_computation.3 | async-start | bytes 4718592 | tf_op jit(solution)/shard_map/all_gather | solution.py:13
  63.1 31.9 %reduce-scatter.2.cloned.1.call-start = ((), (), s32[]{:S(2)}) async-start(), calls=%async_computation.4 | async-start | bytes 1572864 | tf_op jit(solution)/shard_map/reduce_scatter | solution.py:25
  85.2 17.9 %copy-start = (s32[4,8]{1,0:T(4,128)S(1)}, s32[4,8]{1,0:T(4,128)}, u32[]{:S(2)}) copy-start(s32[4,8]{1,0:T(4,128)} %param.8) | copy-start | bytes 388
  85.2 17.9 %copy-start.1 = (f32[64]{0:T(128)S(1)}, f32[64]{0:T(128)}, u32[]{:S(2)}) copy-start(f32[64]{0:T(128)} %param.9) | copy-start | bytes 772
  97.3 20.7 %all-to-all-start = ((f32[1,512,256]{2,0,1:T(1,128)}), f32[1,512,256]{2,0,1:T(1,128)S(1)}, u32[]{:S(2)}, u32[]{:S(2)}) async-start(f32[1,512,256]{2,0,1:T(1,128)} %copy.13), calls=%async_computation.1 | async-start | bytes 1048576 | tf_op jit(solution)/shard_map/all_to_all | solution.py:29
Sparse Core Ops, SparseCore 0:
  9.5 46.8 all-gather.2
  63.2 10.4 all-gather.4
  85.3 9.5 reduce-scatter.1
where the time goes:
time: 126 us
  waiting for transfers between devices  83.6 us (66%)
  between operations  13.1 us (10%)
  matrix products  12.3 us (10%)
  local copies, waits for them, and re-layouts  8.37 us (7%)
  starting transfers between devices  5.84 us (5%)
  other arithmetic  2.9 us (2%)
    all_gather x1, waiting for transfers between devices, body(): own_rows = lax.all_gather(densities, 'freq', axis=1, tiled=True)  47.8 us
    all_to_all x1, waiting for transfers between devices, body(): lax.all_to_all(halves[None], 'freq', split_axis=1, concat_axis=0, tiled=T...  14.8 us
    dot_general x1, matrix products, body(): lax.dot_general(own_rows, product, (((0,), (0,)), ((), ())), preferred_el...  11.5 us
    all_gather x1, waiting for transfers between devices, body(): lax.all_gather(own_rows, 'gvec', axis=0, tiled=True)  10.6 us
    reduce_scatter x1, waiting for transfers between devices, body(): halves = lax.psum_scatter(kernel, 'gvec', scatter_dimension=1, tiled=True)  9.73 us
    all_to_all x1, starting transfers between devices, body(): lax.all_to_all(halves[None], 'freq', split_axis=1, concat_axis=0, tiled=T...  5.76 us
    gather x1, local copies, waits for them, and re-layouts, body(): own_rows = jnp.take(own_rows, pair_order, axis=1)  5.21 us
  transfers between devices with their start and end apart: 4, of which 4 were waited for; matrix products, arithmetic and copies ran while one was open for 1% of the time, Pallas kernels for 0%

commit v1 on v0

v1 whole, which is shorter than its diff:
```python
import functools

import jax
import jax.numpy as jnp
from jax import lax
from jax.experimental import pallas as pl
from jax.experimental.pallas import tpu as pltpu
from jax.sharding import PartitionSpec as P

MESH = pl.DeviceIdType.MESH
F32 = jnp.float32
BF16 = jnp.bfloat16
NT = (((1,), (1,)), ((), ()))


def kernel(
    n, chunks, screened, dens, order, quad_index, quad_table, out,
    w_buf, x_buf, e_buf, acc, p_buf, perm, k_send, k_peer, k_own, k_red, rows_in,
    w_sem, ring_send, ring_recv, pair_send, pair_recv, half_send, half_recv, out_send, out_recv,
):
    rows, per = dens.shape
    pairs = n * per
    half = pairs // 2
    mid = n // 2
    width = rows // chunks
    me = lax.axis_index("freq")
    core = lax.axis_index("gvec")
    peer = 1 - core

    def index_at(position):
        fold = position // mid
        return (1 - fold) * (2 * position) + fold * (2 * (n - 1 - position) + 1)

    odd = me % 2
    place = (1 - odd) * (me // 2) + odd * (n - 1 - me // 2)
    right = index_at((place + 1) % n)
    left = index_at((place + n - 1) % n)

    barrier = pltpu.get_barrier_semaphore()
    pl.semaphore_signal(barrier, inc=1, device_id={"freq": left}, device_id_type=MESH)
    pl.semaphore_signal(barrier, inc=1, device_id={"freq": right}, device_id_type=MESH)
    pl.semaphore_signal(barrier, inc=1, device_id={"gvec": peer}, device_id_type=MESH)

    def w_copy(c, h):
        columns = pl.ds(h * rows + c * width, width)
        return pltpu.make_async_copy(
            screened.at[0, :, columns], w_buf.at[c, h], w_sem.at[c, h]
        )

    for c in range(chunks):
        for h in range(2):
            w_copy(c, h).start()

    eye = (
        lax.broadcasted_iota(jnp.int32, (per, per), 0)
        == lax.broadcasted_iota(jnp.int32, (per, per), 1)
    ).astype(F32).astype(BF16)
    mine = pl.ds(pl.multiple_of(me * per, per), per)
    for c in range(chunks):
        block = lax.dot_general(
            eye, dens[c * width:(c + 1) * width, :], NT, preferred_element_type=F32
        )
        x_buf[c, core, mine, :] = block.astype(BF16)

    def ring_copy(c, slot, origin, target):
        ref = x_buf.at[c, core, pl.ds(pl.multiple_of(origin * per, per), per), :]
        return pltpu.make_async_remote_copy(
            src_ref=ref, dst_ref=ref, send_sem=ring_send.at[c, slot],
            recv_sem=ring_recv.at[c, slot], device_id={"freq": target}, device_id_type=MESH,
        )

    def pair_copy(c, slot, origin, side):
        ref = x_buf.at[c, side, pl.ds(pl.multiple_of(origin * per, per), per), :]
        return pltpu.make_async_remote_copy(
            src_ref=ref, dst_ref=ref, send_sem=pair_send.at[c, slot],
            recv_sem=pair_recv.at[c, slot], device_id={"gvec": peer}, device_id_type=MESH,
        )

    def reach(c):
        ahead = mid if c % 2 == 0 else mid - 1
        return ahead, n - 1 - ahead

    pl.semaphore_wait(barrier, 3)
    for c in range(chunks):
        ring_copy(c, 0, me, right).start()
        ring_copy(c, mid, me, left).start()
    for c in range(chunks):
        pair_copy(c, 0, me, core).start()

    one_hot = (
        lax.broadcasted_iota(jnp.int32, (pairs, pairs), 0) == order[...]
    ).astype(F32)
    perm[...] = one_hot.T.astype(BF16)

    def take(c, d):
        ahead, behind = reach(c)
        if d <= ahead:
            origin = index_at((place + n - d) % n)
            ring_copy(c, d - 1, origin, right).wait_recv()
            if d < ahead:
                ring_copy(c, d, origin, right).start()
            pair_copy(c, d, origin, core).start()
        if d <= behind:
            origin = index_at((place + d) % n)
            ring_copy(c, mid + d - 1, origin, left).wait_recv()
            if d < behind:
                ring_copy(c, mid + d, origin, left).start()
            pair_copy(c, mid + d, origin, core).start()

    def from_peer(c):
        ahead, behind = reach(c)
        pair_copy(c, 0, me, peer).wait_recv()
        for d in range(1, ahead + 1):
            pair_copy(c, d, index_at((place + n - d) % n), peer).wait_recv()
        for d in range(1, behind + 1):
            pair_copy(c, mid + d, index_at((place + d) % n), peer).wait_recv()

    tile = rows // 3 if rows % 48 == 0 else rows

    def multiply(c):
        for h in range(2):
            w_copy(c, h).wait()
            e_buf[h, :, c * width:(c + 1) * width] = jnp.dot(
                perm[...], x_buf[c, h], preferred_element_type=F32
            ).astype(BF16)

        def step(t, _):
            at = pl.ds(pl.multiple_of(t * tile, tile), tile)
            total = sum(
                lax.dot_general(
                    w_buf[c, h, at, :], e_buf[h, :, c * width:(c + 1) * width], NT,
                    preferred_element_type=F32,
                )
                for h in range(2)
            )
            if c > 0:
                total = total + acc[at, :]
            if c < chunks - 1:
                acc[at, :] = total
            else:
                total = total.astype(BF16)
                p_buf[0, at, :] = total[:, :half]
                p_buf[1, at, :] = total[:, half:]
            return 0

        lax.fori_loop(0, rows // tile, step, 0)

    for d in range(1, mid):
        for c in range(chunks):
            take(c, d)
    for c in range(chunks):
        take(c, mid)
    for c in range(chunks):
        from_peer(c)
        multiply(c)

    def half_copy(i):
        return pltpu.make_async_remote_copy(
            src_ref=k_send.at[i], dst_ref=k_peer.at[i], send_sem=half_send.at[i],
            recv_sem=half_recv.at[i], device_id={"gvec": peer}, device_id_type=MESH,
        )

    def out_copy(target, slot):
        return pltpu.make_async_remote_copy(
            src_ref=k_red.at[pl.ds(pl.multiple_of(target * per, per), per), :],
            dst_ref=rows_in.at[me], send_sem=out_send.at[slot], recv_sem=out_recv.at[me],
            device_id={"freq": target}, device_id_type=MESH,
        )

    near = me // mid
    blocks = (1 - near, near)
    local = me % mid

    for i, b in enumerate(blocks):
        at = pl.ds(pl.multiple_of(b * half, half), half)
        k_send[i] = jnp.dot(e_buf[core, at, :], p_buf[peer], preferred_element_type=F32)
        half_copy(i).start()
    for i, b in enumerate(blocks):
        at = pl.ds(pl.multiple_of(b * half, half), half)
        k_own[i] = jnp.dot(e_buf[core, at, :], p_buf[core], preferred_element_type=F32)
    targets = []
    for i, b in enumerate(blocks):
        at = pl.ds(pl.multiple_of(b * half, half), half)
        half_copy(i).wait_recv()
        k_red[at, :] = (k_own[i] + k_peer[i]).astype(BF16)
        for t in range(i, mid):
            target = b * mid + (local + t) % mid
            out_copy(target, len(targets)).start()
            targets.append(target)
    rows_in[me] = k_red[mine, :]

    for t in range(1, n):
        source = (me + t) % n
        pltpu.make_async_remote_copy(
            src_ref=rows_in.at[source], dst_ref=rows_in.at[source],
            send_sem=out_send.at[0], recv_sem=out_recv.at[source],
            device_id={"freq": source}, device_id_type=MESH,
        ).wait_recv()
    for o in range(out.shape[0]):
        out[o] = sum(
            quad_table[quad_index[o, f]] * rows_in[f].astype(F32) for f in range(n)
        )

    for c in range(chunks):
        ahead, behind = reach(c)
        for d in range(ahead):
            ring_copy(c, d, me, right).wait_send()
        for d in range(behind):
            ring_copy(c, mid + d, me, left).wait_send()
        pair_copy(c, 0, me, core).wait_send()
        for d in range(1, ahead + 1):
            pair_copy(c, d, me, core).wait_send()
        for d in range(1, behind + 1):
            pair_copy(c, mid + d, me, core).wait_send()
    for i in range(2):
        half_copy(i).wait_send()
    for slot, target in enumerate(targets):
        out_copy(target, slot).wait_send()


def body(n, screened, densities, pair_order, quad_index, quad_table):
    rows, per = densities.shape
    pairs = n * per
    half = pairs // 2
    chunks = next(c for c in (4, 3, 2, 1) if rows % (c * 128) == 0 or c == 1)
    width = rows // chunks
    energies = quad_index.shape[0]
    slots = n + 1
    dma = pltpu.SemaphoreType.DMA
    vmem = pl.BlockSpec(memory_space=pltpu.VMEM)
    smem = pl.BlockSpec(memory_space=pltpu.SMEM)
    return pl.pallas_call(
        functools.partial(kernel, n, chunks),
        out_shape=jax.ShapeDtypeStruct((energies, per, half), F32),
        in_specs=[pl.BlockSpec(memory_space=pl.ANY), vmem, vmem, smem, smem],
        out_specs=vmem,
        scratch_shapes=[
            pltpu.VMEM((chunks, 2, rows, width), BF16),
            pltpu.VMEM((chunks, 2, pairs, width), BF16),
            pltpu.VMEM((2, pairs, rows), BF16),
            pltpu.VMEM((rows, pairs), F32),
            pltpu.VMEM((2, rows, half), BF16),
            pltpu.VMEM((pairs, pairs), BF16),
            pltpu.VMEM((2, half, half), F32),
            pltpu.VMEM((2, half, half), F32),
            pltpu.VMEM((2, half, half), F32),
            pltpu.VMEM((pairs, half), BF16),
            pltpu.VMEM((n, per, half), BF16),
            dma((chunks, 2)),
            dma((chunks, slots)), dma((chunks, slots)),
            dma((chunks, slots)), dma((chunks, slots)),
            dma((2,)), dma((2,)), dma((n,)), dma((n,)),
        ],
        compiler_params=pltpu.CompilerParams(
            collective_id=0, has_side_effects=True, vmem_limit_bytes=60 * 1024 * 1024
        ),
    )(screened, densities, pair_order[None, :], quad_index, quad_table)


def solution(mesh):
    placed = (P(("groups", "freq"), "gvec", None), P(("groups", "gvec"), "freq"), P(), P(), P())
    return jax.shard_map(
        functools.partial(body, mesh.shape["freq"]), mesh=mesh, in_specs=placed,
        out_specs=P("groups", "freq", "gvec"), check_vma=False,
    )
```

time: 126 us -> 52.9 us (0.42)
  waiting for transfers between devices: 83.6 us -> 0 us
  Pallas kernels: 0 us -> 49.2 us
  between operations: 13.1 us -> 0.01 us
  matrix products: 12.3 us -> 0 us
  starting transfers between devices: 5.84 us -> 0 us
  local copies, waits for them, and re-layouts: 8.37 us -> 3.51 us
  other arithmetic: 2.9 us -> 0 us
    all_gather x2 -> x0, waiting for transfers between devices: 58.4 us -> none  [the longest x1 47.8 us: body(): own_rows = lax.all_gather(densities, 'freq', axis=1, tiled=True)]
    pallas_call x0 -> x1, Pallas kernels: none -> 49.2 us  [body(): pl.pallas_call(functools.partial(kernel, n, chunks), out_shape=jax.ShapeD...]
    all_to_all x1 -> x0, waiting for transfers between devices: 14.8 us -> none  [body(): lax.all_to_all(halves[None], 'freq', split_axis=1, concat_axis=0, tiled=T...]
    dot_general x2 -> x0, matrix products: 12.3 us -> none  [the longest x1 11.5 us: body(): lax.dot_general(own_rows, product, (((0,), (0,)), ((), ())), preferred_el...]
    reduce_scatter x1 -> x0, waiting for transfers between devices: 9.73 us -> none  [body(): halves = lax.psum_scatter(kernel, 'gvec', scatter_dimension=1, tiled=True)]
    all_to_all x1 -> x0, starting transfers between devices: 5.76 us -> none  [body(): lax.all_to_all(halves[None], 'freq', split_axis=1, concat_axis=0, tiled=T...]
    gather x1 -> x0, local copies, waits for them, and re-layouts: 5.21 us -> none  [body(): own_rows = jnp.take(own_rows, pair_order, axis=1)]
    unnamed x5 -> x2, local copies, waits for them, and re-layouts: 0.04 us -> 3.51 us
  transfers between devices with their start and end apart: 4 -> 0, of which waited for: 4 -> 0; matrix products, arithmetic and copies ran while one was open for 1% -> 0% of each run, Pallas kernels for 0% -> 0%
where the time goes in v1:
time: 52.9 us; the launch traced here: 52.7 us
  Pallas kernels  49.2 us (93%)
  local copies, waits for them, and re-layouts  3.51 us (7%)
    pallas_call x1, Pallas kernels, body(): pl.pallas_call(functools.partial(kernel, n, chunks), out_shape=jax.ShapeD...  49.2 us
    unnamed x2, local copies, waits for them, and re-layouts  3.51 us

profile of v1, /device:TPU:0, one launch (start us, length us, event | category | flops | bytes accessed | tf_op | source)
XLA Modules:
  0.0 52.7 jit_solution(4555966286079025828)
XLA Ops:
  0.0 1.8 %copy.6.dens = bf16[1536,64]{1,0:T(8,128)(2,1)} copy(bf16[1536,64]{0,1:T(8,128)(2,1)} %param.6) | data formatting | bytes 393216 | tf_op args[1]
  1.8 49.2 %shard_map.55 = f32[4,64,256]{2,1,0:T(8,128)} custom-call(bf16[1,1536,3072]{2,1,0:T(8,128)(2,1)} %screened.1, bf16[1536,64]{1,0:T(8,128)(2,1)} %copy.6.dens, s32[1,512]{1,0:T(1,128)} %bitcast.1, s32[4,8]{1,0:T(4,128)} %quad_index.1, f32[64]{0:T(128)} %quad_table.1), custom_call_target="tpu_custom_call" | custom-call | tf_op jit(solution)/shard_map/pallas_call | solution.py:232
  51.0 1.7 %copy.8 = f32[4,64,256]{2,1,0:T(8,128)} copy(f32[4,64,256]{2,1,0:T(8,128)} %shard_map.55) | data formatting | bytes 524288

commit v2 on v1

v2 whole, which is shorter than its diff:
```python
import functools

import jax
import jax.numpy as jnp
from jax import lax
from jax.experimental import pallas as pl
from jax.experimental.pallas import tpu as pltpu
from jax.sharding import PartitionSpec as P

MESH = pl.DeviceIdType.MESH
F32 = jnp.float32
BF16 = jnp.bfloat16
NT = (((1,), (1,)), ((), ()))


def kernel(
    n, chunks, screened, dens, order, quad_index, quad_table, out,
    w_buf, x_buf, e_buf, acc, pa_buf, p_buf, perm, order_rows, k_send, k_peer, k_own, k_red, rows_in,
    own_sem, w_sem, ring_send, ring_recv, pair_send, pair_recv, half_send, half_recv, out_send, out_recv,
):
    per, rows = dens.shape
    pairs = n * per
    half = pairs // 2
    mid = n // 2
    width = rows // chunks
    me = lax.axis_index("freq")
    core = lax.axis_index("gvec")
    peer = 1 - core

    def index_at(position):
        fold = position // mid
        return (1 - fold) * (2 * position) + fold * (2 * (n - 1 - position) + 1)

    odd = me % 2
    place = (1 - odd) * (me // 2) + odd * (n - 1 - me // 2)
    right = index_at((place + 1) % n)
    left = index_at((place + n - 1) % n)

    barrier = pltpu.get_barrier_semaphore()
    pl.semaphore_signal(barrier, inc=1, device_id={"freq": left}, device_id_type=MESH)
    pl.semaphore_signal(barrier, inc=1, device_id={"freq": right}, device_id_type=MESH)
    pl.semaphore_signal(barrier, inc=1, device_id={"gvec": peer}, device_id_type=MESH)

    def w_copy(c, h):
        columns = pl.ds(h * rows + c * width, width)
        return pltpu.make_async_copy(
            screened.at[0, :, columns], w_buf.at[c, h], w_sem.at[c, h]
        )

    mine = pl.ds(pl.multiple_of(me * per, per), per)

    def own_copy(c):
        return pltpu.make_async_copy(
            dens.at[:, pl.ds(c * width, width)], x_buf.at[c, core, 0:per, :], own_sem.at[c]
        )

    for c in range(chunks):
        own_copy(c).start()

    def spot(d, side):
        return n - 1 if d == mid else max(0, 2 * d - 1 + side)

    def ring_copy(c, d, side, target):
        return pltpu.make_async_remote_copy(
            src_ref=x_buf.at[c, core, pl.ds(spot(d, side) * per, per), :],
            dst_ref=x_buf.at[c, core, pl.ds(spot(d + 1, side) * per, per), :],
            send_sem=ring_send.at[c, side * mid + d], recv_sem=ring_recv.at[c, side * mid + d],
            device_id={"freq": target}, device_id_type=MESH,
        )

    def pair_copy(c, at, core_from):
        ref = x_buf.at[c, core_from, pl.ds(at * per, per), :]
        return pltpu.make_async_remote_copy(
            src_ref=ref, dst_ref=ref, send_sem=pair_send.at[c, at],
            recv_sem=pair_recv.at[c, at], device_id={"gvec": peer}, device_id_type=MESH,
        )

    def reach(c):
        ahead = mid if c % 2 == 0 else mid - 1
        return ahead, n - 1 - ahead

    for c in range(chunks):
        own_copy(c).wait()
    pl.semaphore_wait(barrier, 3)
    for c in range(chunks):
        ring_copy(c, 0, 0, right).start()
        ring_copy(c, 0, 1, left).start()
    for c in range(chunks):
        pair_copy(c, 0, core).start()
    for c in range(chunks):
        for h in range(2):
            w_copy(c, h).start()

    for at in range(n):
        d, side = (at + 1) // 2, 1 - at % 2
        origin = index_at((place + (d if side else n - d)) % n)
        pair = lax.broadcasted_iota(jnp.int32, (per, pairs), 0) + origin * per
        one_hot = (pair == order[...]).astype(F32)
        order_rows[at * per:(at + 1) * per, :] = one_hot.astype(BF16)
    perm[...] = order_rows[...].astype(F32).T.astype(BF16)

    def take(c, d):
        for side, last, target in zip((0, 1), reach(c), (right, left)):
            if d <= last:
                ring_copy(c, d - 1, side, target).wait_recv()
                if d < last:
                    ring_copy(c, d, side, target).start()
                pair_copy(c, spot(d, side), core).start()

    tile = rows // 2 if rows % 32 == 0 else rows

    def multiply(c, g):
        for at in range(g * mid, (g + 1) * mid):
            pair_copy(c, at, peer).wait_recv()
        if g == 0:
            for h in range(2):
                w_copy(c, h).wait()
        members = slice(g * half, (g + 1) * half)

        def step(t, _):
            at = pl.ds(pl.multiple_of(t * tile, tile), tile)
            total = sum(
                lax.dot_general(
                    w_buf[c, h, at, :], x_buf[c, h, members, :], NT,
                    preferred_element_type=F32,
                )
                for h in range(2)
            )
            if c > 0:
                total = total + acc[g, at, :]
            if c < chunks - 1:
                acc[g, at, :] = total
                return 0
            total = total.astype(BF16)
            for h in range(2):
                part = jnp.dot(
                    total, order_rows[members, h * half:(h + 1) * half],
                    preferred_element_type=F32,
                )
                if g == 0:
                    pa_buf[h, at, :] = part.astype(BF16)
                else:
                    p_buf[h, at, :] = (part + pa_buf[h, at, :].astype(F32)).astype(BF16)
            return 0

        lax.fori_loop(0, rows // tile, step, 0)

    def order_own(c):
        e_buf[:, c * width:(c + 1) * width] = jnp.dot(
            perm[...], x_buf[c, core], preferred_element_type=F32
        ).astype(BF16)

    for d in range(1, mid // 2 + 1):
        for c in range(chunks):
            take(c, d)
    for c in range(chunks):
        multiply(c, 0)
        for d in range(mid // 2 + 1, mid):
            take(c, d)
    for c in range(chunks):
        take(c, mid)
    for c in range(chunks):
        order_own(c)
        multiply(c, 1)

    def half_copy(i):
        return pltpu.make_async_remote_copy(
            src_ref=k_send.at[i], dst_ref=k_peer.at[i], send_sem=half_send.at[i],
            recv_sem=half_recv.at[i], device_id={"gvec": peer}, device_id_type=MESH,
        )

    def out_copy(target, slot):
        return pltpu.make_async_remote_copy(
            src_ref=k_red.at[pl.ds(pl.multiple_of(target * per, per), per), :],
            dst_ref=rows_in.at[me], send_sem=out_send.at[slot], recv_sem=out_recv.at[me],
            device_id={"freq": target}, device_id_type=MESH,
        )

    near = me // mid
    blocks = (1 - near, near)
    local = me % mid

    for i, b in enumerate(blocks):
        at = pl.ds(pl.multiple_of(b * half, half), half)
        k_send[i] = jnp.dot(e_buf[at, :], p_buf[peer], preferred_element_type=F32)
        half_copy(i).start()
    for i, b in enumerate(blocks):
        at = pl.ds(pl.multiple_of(b * half, half), half)
        k_own[i] = jnp.dot(e_buf[at, :], p_buf[core], preferred_element_type=F32)
    targets = []
    for i, b in enumerate(blocks):
        at = pl.ds(pl.multiple_of(b * half, half), half)
        half_copy(i).wait_recv()
        k_red[at, :] = (k_own[i] + k_peer[i]).astype(BF16)
        for t in range(i, mid):
            target = b * mid + (local + t) % mid
            out_copy(target, len(targets)).start()
            targets.append(target)
    rows_in[me] = k_red[mine, :]

    for t in range(1, n):
        source = (me + t) % n
        pltpu.make_async_remote_copy(
            src_ref=rows_in.at[source], dst_ref=rows_in.at[source],
            send_sem=out_send.at[0], recv_sem=out_recv.at[source],
            device_id={"freq": source}, device_id_type=MESH,
        ).wait_recv()
    for o in range(out.shape[0]):
        out[o] = sum(
            quad_table[quad_index[o, f]] * rows_in[f].astype(F32) for f in range(n)
        )

    for c in range(chunks):
        for side, last, target in zip((0, 1), reach(c), (right, left)):
            for d in range(last):
                ring_copy(c, d, side, target).wait_send()
        for at in range(n):
            pair_copy(c, at, core).wait_send()
    for i in range(2):
        half_copy(i).wait_send()
    for slot, target in enumerate(targets):
        out_copy(target, slot).wait_send()


def body(n, screened, densities, pair_order, quad_index, quad_table):
    rows, per = densities.shape
    pairs = n * per
    half = pairs // 2
    chunks = next(c for c in (4, 3, 2, 1) if rows % (c * 128) == 0 or c == 1)
    width = rows // chunks
    energies = quad_index.shape[0]
    dma = pltpu.SemaphoreType.DMA
    hbm = pl.BlockSpec(memory_space=pl.ANY)
    vmem = pl.BlockSpec(memory_space=pltpu.VMEM)
    smem = pl.BlockSpec(memory_space=pltpu.SMEM)
    return pl.pallas_call(
        functools.partial(kernel, n, chunks),
        out_shape=jax.ShapeDtypeStruct((energies, per, half), F32),
        in_specs=[hbm, hbm, vmem, smem, smem],
        out_specs=vmem,
        scratch_shapes=[
            pltpu.VMEM((chunks, 2, rows, width), BF16),
            pltpu.VMEM((chunks, 2, pairs, width), BF16),
            pltpu.VMEM((pairs, rows), BF16),
            pltpu.VMEM((2, rows, half), F32),
            pltpu.VMEM((2, rows, half), BF16),
            pltpu.VMEM((2, rows, half), BF16),
            pltpu.VMEM((pairs, pairs), BF16),
            pltpu.VMEM((pairs, pairs), BF16),
            pltpu.VMEM((2, half, half), F32),
            pltpu.VMEM((2, half, half), F32),
            pltpu.VMEM((2, half, half), F32),
            pltpu.VMEM((pairs, half), BF16),
            pltpu.VMEM((n, per, half), BF16),
            dma((chunks,)), dma((chunks, 2)),
            dma((chunks, n)), dma((chunks, n)),
            dma((chunks, n)), dma((chunks, n)),
            dma((2,)), dma((2,)), dma((n,)), dma((n,)),
        ],
        compiler_params=pltpu.CompilerParams(
            collective_id=0, has_side_effects=True, vmem_limit_bytes=60 * 1024 * 1024
        ),
    )(screened, densities.T, pair_order[None, :], quad_index, quad_table)


def solution(mesh):
    placed = (P(("groups", "freq"), "gvec", None), P(("groups", "gvec"), "freq"), P(), P(), P())
    return jax.shard_map(
        functools.partial(body, mesh.shape["freq"]), mesh=mesh, in_specs=placed,
        out_specs=P("groups", "freq", "gvec"), check_vma=False,
    )
```

time: 52.9 us -> 47.6 us (0.90)
  Pallas kernels: 49.2 us -> 45.7 us
  local copies, waits for them, and re-layouts: 3.51 us -> 1.67 us
    pallas_call x1, Pallas kernels: 49.2 us -> 45.7 us  [body(): pl.pallas_call(functools.partial(kernel, n, chunks), out_shape=jax.ShapeD...]
    unnamed x2 -> x1, local copies, waits for them, and re-layouts: 3.51 us -> 1.67 us
where the time goes in v2:
time: 47.6 us; the launch traced here: 47.4 us
  Pallas kernels  45.7 us (96%)
  local copies, waits for them, and re-layouts  1.67 us (4%)
    pallas_call x1, Pallas kernels, body(): pl.pallas_call(functools.partial(kernel, n, chunks), out_shape=jax.ShapeD...  45.7 us
    unnamed x1, local copies, waits for them, and re-layouts  1.67 us

profile of v2, /device:TPU:0, one launch (start us, length us, event | category | flops | bytes accessed | tf_op | source)
XLA Modules:
  0.0 47.4 jit_solution(8076514751275478089)
XLA Ops:
  0.0 45.7 %shard_map.55 = f32[4,64,256]{2,1,0:T(8,128)} custom-call(bf16[1,1536,3072]{2,1,0:T(8,128)(2,1)} %screened.1, bf16[64,1536]{1,0:T(8,128)(2,1)} %bitcast.2, s32[1,512]{1,0:T(1,128)} %bitcast.3, s32[4,8]{1,0:T(4,128)} %quad_index.1, f32[64]{0:T(128)} %quad_table.1), custom_call_target="tpu_custom_call" | custom-call | tf_op jit(solution)/shard_map/pallas_call | solution.py:236
  45.7 1.7 %copy.7 = f32[4,64,256]{2,1,0:T(8,128)} copy(f32[4,64,256]{2,1,0:T(8,128)} %shard_map.55) | data formatting | bytes 524288
